TPU v7x, 32 devices: a whole 2x2x4 slice. The times are simulated.
32 devices in a mesh: grp: 4 (over y, x), dev: 8 (over z, core).
Axes of the slice: x: 2, y: 2, z: 4, core: 2. Of those that a mesh axis runs over, the one named last changes fastest.
Arguments:
- embeddings: bfloat16 [262144, 256], P(('grp', 'dev'))
- prior_dist: float32 [262144], P(('grp', 'dev')), may hold values from 1 to 3
- seed_ids: int32 [6, 512], replicated, may hold values from 0 to 262143, as said below
Outputs:
- min_dist: float32 [262144], P(('grp', 'dev'))
- group_means: float32 [6, 4], P(None, 'grp')
Inputs may be any that keep to these rules, and one draw needn't show every extreme that they name: `seed_ids`: round r's ids all lie in the rows of group r mod 4, that is from (r mod 4) * 65536 to (r mod 4 + 1) * 65536 - 1; ids may repeat.
All inputs are finite; a program needn't handle non-finite values.
Results may differ from a plain program's by a relative error of at most 0.0003.
Values may be sent and summed in bfloat16 or wider, within the bound.
A program may use at most 64 MiB of HBM per device.

v0:
```python
import jax
import jax.numpy as jnp
from jax import lax
from jax.sharding import PartitionSpec as P


def block_gaps(block, block_norms, centers, seed_norms, feature_dim):
    products = jnp.dot(block, centers.T, preferred_element_type=jnp.float32)
    return jnp.maximum(block_norms[:, None] + seed_norms[None, :] - 2.0 * products, 0.0) / float(
        feature_dim
    )


def body(embeddings, prior_dist, seed_ids):
    row_count, feature_dim = embeddings.shape
    round_count, seed_count = seed_ids.shape
    dev_count = lax.axis_size("dev")
    row_start = (lax.axis_index("grp") * dev_count + lax.axis_index("dev")) * row_count
    offsets = seed_ids - row_start
    inside = (offsets >= 0) & (offsets < row_count)
    picked = jnp.take(embeddings, jnp.clip(offsets, 0, row_count - 1), axis=0)
    picked = jnp.where(inside[:, :, None], picked.astype(jnp.float32), 0.0)
    owned = lax.psum(picked.astype(jnp.bfloat16), "dev")
    summed = lax.psum(owned, "grp")
    centers = [summed[round_index] for round_index in range(round_count)]
    seed_norms = [jnp.sum(jnp.square(center.astype(jnp.float32)), axis=1) for center in centers]
    row_norms = jnp.sum(jnp.square(embeddings.astype(jnp.float32)), axis=1)
    block_rows = min(2048, row_count)
    block_count = row_count // block_rows
    blocks = embeddings.reshape(block_count, block_rows, feature_dim)
    norm_blocks = row_norms.reshape(block_count, block_rows)
    per_round = []
    for round_index in range(round_count):
        center = centers[round_index]
        center_norms = seed_norms[round_index]

        def one_round(pair, center=center, center_norms=center_norms):
            return jnp.min(block_gaps(pair[0], pair[1], center, center_norms, feature_dim), axis=1)

        per_round.append(lax.map(one_round, (blocks, norm_blocks)).reshape(row_count))
    group_total = float(row_count * dev_count)
    current = prior_dist
    collected = []
    for round_index in range(round_count):
        current = jnp.minimum(current, per_round[round_index])
        collected.append(lax.psum(jnp.sum(current), "dev") / group_total)
    means = jnp.stack(collected)
    return (current, means.reshape(round_count, 1))


def solution(mesh):
    placed = (P(("grp", "dev"), None), P(("grp", "dev")), P())
    return jax.shard_map(
        body,
        mesh=mesh,
        in_specs=placed,
        out_specs=(P(("grp", "dev")), P(None, "grp")),
        check_vma=False,
    )
```

profile of v0, /device:TPU:0, one launch (start us, length us, event | category | flops | bytes accessed | tf_op | source)
XLA Modules:
  0.0 242.5 jit_solution(16635363489336066395)
XLA Ops:
  8.0 12.5 %gather_fusion = bf16[3072,256]{1,0:T(8,128)(2,1)S(1)} fusion(bf16[8192,256]{1,0:T(8,128)(2,1)} %param.15, s32[3072]{0:T(1024)S(1)} %broadcast_clamp_fusion), kind=kCustom, calls=%fused_computation | custom fusion | bytes 3158016 | tf_op jit(solution)/shard_map/jit(_take)/gather | solution.py:21
  20.5 2.4 select_convert_fusion
  23.0 64.7 %all-reduce.4.cloned.1.call-done = bf16[6,512,256]{2,1,0:T(8,128)(2,1)} async-done(((bf16[6,512,256]{2,1,0:T(8,128)(2,1)}), bf16[6,512,256]{2,1,0:T(8,128)(2,1)}) %all-reduce.4.cloned.1.call-update) | async-done | bytes 1572880 | tf_op jit(solution)/shard_map/psum | solution.py:23
  87.7 3.3 %multiply_reduce_fusion.6 = f32[8192]{0:T(1024)S(1)} fusion(bf16[8192,256]{1,0:T(8,128)(2,1)} %param.15), kind=kLoop, calls=%fused_computation.31 | loop fusion | flops 6283264 | bytes 4227072 | tf_op jit(solution)/shard_map/reduce_sum | solution.py:27
  91.0 59.7 %all-reduce.6.cloned.1.call-done = bf16[6,512,256]{2,1,0:T(8,128)(2,1)} async-done(((bf16[6,512,256]{2,1,0:T(8,128)(2,1)}), bf16[6,512,256]{2,1,0:T(8,128)(2,1)}) %all-reduce.6.cloned.1.call-update) | async-done | bytes 1572880 | tf_op jit(solution)/shard_map/psum | solution.py:24
  153.1 9.9 %while.62 = (s32[]{:T(128)}, f32[4,2048]{1,0:T(4,128)S(1)}, f32[4,2048]{1,0:T(4,128)S(1)}, f32[512]{0:T(512)S(1)}, bf16[4,2048,256]{2,1,0:T(8,128)(2,1)}, /*inde...) while((s32[]{:T(128)}, f32[4,2048]{1,0:T(4,128)S(1)}, f32[4,2048]{1,0:T(4,128)S(1)}, f32[512]{0:T(512)S(1)}, ...), condition=%wide.region_14.15_spmd, body=%wide.region_12.14_spmd.sunk | while | flops 543160320 | bytes 1362525 | solution.py:40
  153.1 2.3 multiply_reduce_fusion.21
  155.6 2.3 multiply_reduce_fusion.21
  158.1 2.3 multiply_reduce_fusion.21
  160.5 2.3 multiply_reduce_fusion.21
  163.0 9.9 %while.64 = (s32[]{:T(128)}, f32[4,2048]{1,0:T(4,128)S(1)}, f32[4,2048]{1,0:T(4,128)S(1)}, f32[512]{0:T(512)S(1)}, bf16[4,2048,256]{2,1,0:T(8,128)(2,1)}, /*inde...) while((s32[]{:T(128)}, f32[4,2048]{1,0:T(4,128)S(1)}, f32[4,2048]{1,0:T(4,128)S(1)}, f32[512]{0:T(512)S(1)}, ...), condition=%wide.region_22.23_spmd, body=%wide.region_20.22_spmd.sunk | while | flops 543160320 | bytes 1362525 | solution.py:40
  165.5 2.3 multiply_reduce_fusion.23
  168.0 2.3 multiply_reduce_fusion.23
  170.4 2.3 multiply_reduce_fusion.23
  172.9 9.9 %while.60 = (s32[]{:T(128)}, f32[4,2048]{1,0:T(4,128)S(1)}, f32[4,2048]{1,0:T(4,128)S(1)}, f32[512]{0:T(512)S(1)}, bf16[4,2048,256]{2,1,0:T(8,128)(2,1)}, /*inde...) while((s32[]{:T(128)}, f32[4,2048]{1,0:T(4,128)S(1)}, f32[4,2048]{1,0:T(4,128)S(1)}, f32[512]{0:T(512)S(1)}, ...), condition=%wide.region_6.7_spmd, body=%wide.region_4.6_spmd.sunk | while | flops 543160320 | bytes 1362525 | solution.py:40
  172.9 2.3 multiply_reduce_fusion.19
  175.4 2.3 multiply_reduce_fusion.19
  177.9 2.3 multiply_reduce_fusion.19
  180.3 2.3 multiply_reduce_fusion.19
  182.8 9.9 %while.61 = (s32[]{:T(128)}, f32[4,2048]{1,0:T(4,128)S(1)}, f32[4,2048]{1,0:T(4,128)S(1)}, f32[512]{0:T(512)S(1)}, bf16[4,2048,256]{2,1,0:T(8,128)(2,1)}, /*inde...) while((s32[]{:T(128)}, f32[4,2048]{1,0:T(4,128)S(1)}, f32[4,2048]{1,0:T(4,128)S(1)}, f32[512]{0:T(512)S(1)}, ...), condition=%wide.region_10.11_spmd, body=%wide.region_8.10_spmd.sunk | while | flops 543160320 | bytes 1362525 | solution.py:40
  182.8 2.3 multiply_reduce_fusion.20
  185.3 2.3 multiply_reduce_fusion.20
  187.7 2.3 multiply_reduce_fusion.20
  190.2 2.3 multiply_reduce_fusion.20
  192.7 9.8 %while.63 = (s32[]{:T(128)}, f32[4,2048]{1,0:T(4,128)S(1)}, f32[4,2048]{1,0:T(4,128)S(1)}, f32[512]{0:T(512)S(1)}, bf16[4,2048,256]{2,1,0:T(8,128)(2,1)}, /*inde...) while((s32[]{:T(128)}, f32[4,2048]{1,0:T(4,128)S(1)}, f32[4,2048]{1,0:T(4,128)S(1)}, f32[512]{0:T(512)S(1)}, ...), condition=%wide.region_18.19_spmd, body=%wide.region_16.18_spmd.sunk | while | flops 543160320 | bytes 1362525 | solution.py:40
  192.7 2.3 multiply_reduce_fusion.22
  197.6 2.3 multiply_reduce_fusion.22
  202.6 9.8 %while.65 = (s32[]{:T(128)}, f32[4,2048]{1,0:T(4,128)S(1)}, f32[4,2048]{1,0:T(4,128)S(1)}, f32[512]{0:T(512)S(1)}, bf16[4,2048,256]{2,1,0:T(8,128)(2,1)}, /*inde...) while((s32[]{:T(128)}, f32[4,2048]{1,0:T(4,128)S(1)}, f32[4,2048]{1,0:T(4,128)S(1)}, f32[512]{0:T(512)S(1)}, ...), condition=%wide.region_26.27_spmd, body=%wide.region_24.26_spmd.sunk | while | flops 543160320 | bytes 1362525 | solution.py:40
  202.6 2.3 multiply_reduce_fusion.24
  205.1 2.3 multiply_reduce_fusion.24
  207.5 2.3 multiply_reduce_fusion.24
  214.4 16.9 %all-reduce = (f32[]{:T(128)}, f32[]{:T(128)}, f32[]{:T(128)}, f32[]{:T(128)}, f32[]{:T(128)}, /*index=5*/f32[]{:T(128)}) all-reduce(f32[]{:T(128)} %get-tuple-element.300, f32[]{:T(128)} %get-tuple-element.302, f32[]{:T(128)} %get-tuple-element.303, f32[]{:T(128)} %get-tuple-element.207, ...), channel_id=1, replica_groups=mesh['grp'=4,'dev'=8] {'dev'}, use_global_device_ids=true, to_apply=%region_28.29 | all-reduce | flops 6 | bytes 48 | tf_op jit(solution)/shard_map/psum | solution.py:46
  (81 shorter events, 18.4 us)
Async XLA Ops:
  7.2 80.5 %all-reduce.4.cloned.1.call-start = ((), (), s32[]{:S(2)}) async-start(), calls=%async_computation | async-start | bytes 3145728 | tf_op jit(solution)/shard_map/psum | solution.py:23
  22.9 127.8 %all-reduce.6.cloned.1.call-start = ((), (), s32[]{:S(2)}) async-start(), calls=%async_computation.1 | async-start | bytes 3145728 | tf_op jit(solution)/shard_map/psum | solution.py:24
  150.7 1.9 copy-start
  202.5 9.9 %copy-start.1 = (f32[8192]{0:T(1024)S(1)}, f32[8192]{0:T(1024)}, u32[]{:S(2)}) copy-start(f32[8192]{0:T(1024)} %param.16) | copy-start | bytes 98308
Sparse Core Ops, SparseCore 0:
  23.1 64.5 all-reduce.3
  90.7 59.9 all-reduce.5
where the time goes:
time: 244 us; the launch traced here: 243 us
  waiting for transfers between devices  124 us (51%)
  matrix products  54.8 us (22%)
  local copies, waits for them, and re-layouts  18.5 us (8%)
  between operations  18 us (7%)
  blocking collectives  16.9 us (7%)
  other arithmetic  8.89 us (4%)
    psum x1, waiting for transfers between devices, body(): owned = lax.psum(picked.astype(jnp.bfloat16), 'dev')  64.7 us
    psum x1, waiting for transfers between devices, body(): summed = lax.psum(owned, 'grp')  59.7 us
    dot_general x24, matrix products, block_gaps(): products = jnp.dot(block, centers.T, preferred_element_type=jnp.float32)  54.8 us
    psum x1, blocking collectives, body(): collected.append(lax.psum(jnp.sum(current), 'dev') / group_total)  16.9 us
    gather x1, local copies, waits for them, and re-layouts, body(): picked = jnp.take(embeddings, jnp.clip(offsets, 0, row_count - 1), axis=0)  12.5 us
  transfers between devices with their start and end apart: 2, of which 2 were waited for; matrix products, arithmetic and copies ran while one was open for 1% of the time, Pallas kernels for 0%

commit v1 on v0

v1 whole, which is shorter than its diff:
```python
import functools

import jax
import jax.numpy as jnp
from jax import lax
from jax.experimental import pallas as pl
from jax.experimental.pallas import tpu as pltpu
from jax.sharding import PartitionSpec as P

MESH = pl.DeviceIdType.MESH
LOAD_CHUNKS = 8
TILE = 256
NT = (((1,), (1,)), ((), ()))


def split_square(x):
    square = jnp.square(x)
    high = square.astype(jnp.bfloat16)
    return high, (square - high.astype(jnp.float32)).astype(jnp.bfloat16)


def kernel(
    sizes, ids, prior, e_hbm, dist, means,
    e, ef, pick, out_half, own_half, pin, half, zin, cent, snb, hm, rn, part, parts,
    load_sem, p_sem, rs_sem, ag_sem, grp_sem, fwd_sem, mean_sem,
):
    groups, devs, rounds, seeds, rows, width = sizes
    chips = devs // 2
    half_rows = seeds // 2
    piece = half_rows // chips
    slots = (rounds + groups - 1) // groups
    g, d = lax.axis_index("grp"), lax.axis_index("dev")
    c, h = d // 2, d % 2
    partner = c * 2 + (1 - h)
    row_start = (g * devs + d) * rows
    chunk = rows // LOAD_CHUNKS

    def load(i):
        at = pl.ds(i * chunk, chunk)
        return pltpu.make_async_copy(e_hbm.at[at], e.at[at], load_sem.at[i])

    for i in range(LOAD_CHUNKS):
        load(i).start()

    barrier = pltpu.get_barrier_semaphore()
    for o in range(1, devs):
        pl.semaphore_signal(barrier, inc=1, device_id=(g, (d + o) % devs), device_id_type=MESH)

    def peer(o):
        total, base = 0, 1
        while base < groups:
            total = total + (((g // base) % 2 + (o // base) % 2) % 2) * base
            base *= 2
        return total

    for o in range(1, groups):
        pl.semaphore_signal(barrier, inc=1, device_id=(peer(o), d), device_id_type=MESH)

    for i in range(LOAD_CHUNKS):
        load(i).wait()

        @pl.loop(0, chunk // 64)
        def _(t):
            at = pl.ds(pl.multiple_of(i * chunk + t * 64, 64), 64)
            ef[at, :] = e[at, :].astype(jnp.float32)

    def gather(slot, which, dst):
        r = g + groups * slot

        @pl.loop(0, half_rows // 16)
        def _(b):
            for q in range(16):
                i = b * 16 + q
                offset = ids[r, which * half_rows + i] - row_start
                inside = (offset >= 0) & (offset < rows)
                row = ef[pl.ds(jnp.where(inside, offset, 0), 1), :]
                pick[pl.ds(i, 1), :] = jnp.where(inside, row, 0.0)

        dst[slot] = pick[0:half_rows, :].astype(jnp.bfloat16)

    def send(src, dst, sem, k, j, device):
        return pltpu.make_async_remote_copy(
            src_ref=src, dst_ref=dst, send_sem=sem.at[0, k, j], recv_sem=sem.at[1, k, j],
            device_id=device, device_id_type=MESH,
        )

    def to_partner(k):
        return send(out_half.at[k], pin.at[k], p_sem, k, 0, (g, partner))

    def scatter(k, o):
        target = (c + o) % chips
        return send(half.at[k, target], zin.at[k, o], rs_sem, k, o, (g, target * 2 + h))

    def spread(k, o):
        block = cent.at[g + groups * k, h, c]
        return send(block, block, ag_sem, k, o, (g, ((c + o) % chips) * 2 + h))

    def across(k, o, origin=None):
        block = cent.at[(g if origin is None else origin) + groups * k, h]
        return send(block, block, grp_sem, k, o, (peer(o), d))

    def forward(k, o):
        block = cent.at[peer(o) + groups * k, h]
        return send(block, block, fwd_sem, k, o, (g, partner))

    def if_held(k, o, f):
        if groups * (k + 1) <= rounds:
            f()
        else:
            pl.when(peer(o) + groups * k < rounds)(f)

    first = True
    for k in range(slots):
        def start_slot(k=k, first=first):
            gather(k, 1 - h, out_half)
            if first:
                pl.semaphore_wait(barrier, devs - 1 + groups - 1)
            to_partner(k).start()
            gather(k, h, own_half)

        if_held(k, 0, start_slot)
        first = False

    for k in range(slots):
        def reduce_pair(k=k):
            to_partner(k).wait_recv()
            both = own_half[k] + pin[k]
            half[k] = both.reshape(chips, piece, width)
            for o in range(1, chips):
                scatter(k, o).start()

        if_held(k, 0, reduce_pair)

    ones_row = jnp.ones((8, width), jnp.bfloat16)

    @pl.loop(0, rows // TILE)
    def _(t):
        at = pl.ds(pl.multiple_of(t * TILE, TILE), TILE)
        high, low = split_square(ef[at, :])
        total = lax.dot_general(ones_row, high, NT, preferred_element_type=jnp.float32)
        total += lax.dot_general(ones_row, low, NT, preferred_element_type=jnp.float32)
        for q in range(TILE // 128):
            rn[t * (TILE // 128) + q] = total[:, q * 128 : (q + 1) * 128]

    for k in range(slots):
        def reduce_chips(k=k):
            total = half[k, c]
            for o in range(1, chips):
                scatter(k, o).wait_recv()
                total += zin[k, o]
            cent[g + groups * k, h, c] = total
            for o in range(1, chips):
                spread(k, o).start()

        if_held(k, 0, reduce_chips)

    for k in range(slots):
        def share(k=k):
            for o in range(1, chips):
                spread(k, o).wait_recv()
            for o in range(1, groups):
                across(k, o).start()
            forward(k, 0).start()

        if_held(k, 0, share)

    ones_col = jnp.ones((width, 128), jnp.bfloat16)

    def compute(r):
        centers = cent[r].reshape(seeds, width)
        high, low = split_square(centers.astype(jnp.float32))
        norms = jnp.dot(high, ones_col, preferred_element_type=jnp.float32)
        norms += jnp.dot(low, ones_col, preferred_element_type=jnp.float32)
        snb[...] = 0.5 * norms

        @pl.loop(0, rows // TILE)
        def _(t):
            at = pl.multiple_of(t * TILE, TILE)
            block = e[pl.ds(at, TILE), :]
            products = lax.dot_general(
                cent[r].reshape(seeds, width), block, NT, preferred_element_type=jnp.float32
            )
            for q in range(TILE // 128):
                score = products[:, q * 128 : (q + 1) * 128] - snb[...]
                hm[r, t * (TILE // 128) + q] = jnp.max(score.reshape(seeds // 8, 8, 128), axis=0)

    items = [(k, o) for k in range(slots) for o in range(groups)]

    def relay(k, o):
        def f():
            across(k, o, peer(o)).wait_recv()
            forward(k, o).start()

        if o:
            if_held(k, o, f)

    def finish(k, o):
        def f():
            forward(k, o).wait_recv()
            compute(peer(o) + groups * k)

        if_held(k, o, f)

    for n, (k, o) in enumerate(items):
        if n + 1 < len(items):
            relay(*items[n + 1])
        finish(k, o)

    current = prior[...]
    norms = jnp.max(rn[...], axis=1)
    sums = []
    for r in range(rounds):
        best = jnp.max(hm[r], axis=1)
        gap = jnp.maximum(norms - 2.0 * best, 0.0) * (1.0 / width)
        current = jnp.minimum(current, gap)
        sums.append(jnp.sum(current, axis=0, keepdims=True))
    if rounds < 8:
        sums.append(jnp.zeros((8 - rounds, 128), jnp.float32))
    part[...] = jnp.concatenate(sums, axis=0)
    dist[...] = current

    def send_part(o):
        return send(part, parts.at[o], mean_sem, 0, o, (g, (d + o) % devs))

    for o in range(1, devs):
        send_part(o).start()
    total = part[...]
    for o in range(1, devs):
        send_part(o).wait_recv()
        total += parts[o]
    means[...] = jnp.broadcast_to(
        jnp.sum(total, axis=1, keepdims=True) / float(rows * devs), (8, 128)
    )

    for o in range(1, devs):
        send_part(o).wait_send()
    for k in range(slots):
        def drain(k=k):
            to_partner(k).wait_send()
            for o in range(1, chips):
                scatter(k, o).wait_send()
                spread(k, o).wait_send()
            for o in range(1, groups):
                across(k, o).wait_send()

        if_held(k, 0, drain)
        for o in range(groups):
            if_held(k, o, lambda k=k, o=o: forward(k, o).wait_send())


def body(embeddings, prior_dist, seed_ids):
    rows, width = embeddings.shape
    rounds, seeds = seed_ids.shape
    groups, devs = lax.axis_size("grp"), lax.axis_size("dev")
    chips = devs // 2
    slots = (rounds + groups - 1) // groups
    half_rows = seeds // 2
    piece = half_rows // chips
    bf16, f32 = jnp.bfloat16, jnp.float32
    vmem = pl.BlockSpec(memory_space=pltpu.VMEM)
    dist, means = pl.pallas_call(
        functools.partial(kernel, (groups, devs, rounds, seeds, rows, width)),
        out_shape=(
            jax.ShapeDtypeStruct((rows // 128, 128), f32),
            jax.ShapeDtypeStruct((8, 128), f32),
        ),
        in_specs=[
            pl.BlockSpec(memory_space=pltpu.SMEM),
            vmem,
            pl.BlockSpec(memory_space=pl.ANY),
        ],
        out_specs=(vmem, vmem),
        scratch_shapes=[
            pltpu.VMEM((rows, width), bf16),
            pltpu.VMEM((rows + 8, width), f32),
            pltpu.VMEM((half_rows + 8, width), f32),
            pltpu.VMEM((slots, half_rows, width), bf16),
            pltpu.VMEM((slots, half_rows, width), bf16),
            pltpu.VMEM((slots, half_rows, width), bf16),
            pltpu.VMEM((slots, chips, piece, width), bf16),
            pltpu.VMEM((slots, chips, piece, width), bf16),
            pltpu.VMEM((rounds, 2, chips, piece, width), bf16),
            pltpu.VMEM((seeds, 128), f32),
            pltpu.VMEM((rounds, rows // 128, 8, 128), f32),
            pltpu.VMEM((rows // 128, 8, 128), f32),
            pltpu.VMEM((8, 128), f32),
            pltpu.VMEM((devs, 8, 128), f32),
            pltpu.SemaphoreType.DMA((LOAD_CHUNKS,)),
            pltpu.SemaphoreType.DMA((2, slots, 1)),
            pltpu.SemaphoreType.DMA((2, slots, chips)),
            pltpu.SemaphoreType.DMA((2, slots, chips)),
            pltpu.SemaphoreType.DMA((2, slots, groups)),
            pltpu.SemaphoreType.DMA((2, slots, groups)),
            pltpu.SemaphoreType.DMA((2, 1, devs)),
        ],
        compiler_params=pltpu.CompilerParams(
            collective_id=0, has_side_effects=True, vmem_limit_bytes=56 * 1024 * 1024
        ),
        name="seed_rounds",
    )(seed_ids, prior_dist.reshape(rows // 128, 128), embeddings)
    return dist.reshape(rows), means[:rounds, :1]


def solution(mesh):
    placed = (P(("grp", "dev"), None), P(("grp", "dev")), P())
    return jax.shard_map(
        body,
        mesh=mesh,
        in_specs=placed,
        out_specs=(P(("grp", "dev")), P(None, "grp")),
        check_vma=False,
    )
```

time: 244 us -> 94.6 us (0.39)
  waiting for transfers between devices: 124 us -> 0 us
  Pallas kernels: 0 us -> 91 us
  matrix products: 54.8 us -> 0 us
  between operations: 18 us -> 0.64 us
  blocking collectives: 16.9 us -> 0 us
  local copies, waits for them, and re-layouts: 18.5 us -> 2.64 us
  other arithmetic: 8.89 us -> 0 us
    psum x2 -> x0, waiting for transfers between devices: 124 us -> none  [the longest x1 64.7 us: body(): owned = lax.psum(picked.astype(jnp.bfloat16), 'dev')]
    pallas_call x0 -> x1, Pallas kernels: none -> 91 us  [body(): pl.pallas_call(functools.partial(kernel, (groups, devs, rounds, seeds, ro...]
    dot_general x24 -> x0, matrix products: 54.8 us -> none  [block_gaps(): products = jnp.dot(block, centers.T, preferred_element_type=jnp.float32)]
    psum x1 -> x0, blocking collectives: 16.9 us -> none  [body(): collected.append(lax.psum(jnp.sum(current), 'dev') / group_total)]
    gather x1 -> x0, local copies, waits for them, and re-layouts: 12.5 us -> none  [body(): picked = jnp.take(embeddings, jnp.clip(offsets, 0, row_count - 1), axis=0)]
    reduce_sum x4 -> x0, other arithmetic: 5.78 us -> none  [the longest x1 3.34 us: body(): row_norms = jnp.sum(jnp.square(embeddings.astype(jnp.float32)), axis=1)]
    dynamic_update_slice x24 -> x0, local copies, waits for them, and re-layouts: 3.12 us -> none  [body(): lax.map(one_round, (blocks, norm_blocks)).reshape(row_count)]
  transfers between devices with their start and end apart: 2 -> 0, of which waited for: 2 -> 0; matrix products, arithmetic and copies ran while one was open for 1% -> 0% of each run, Pallas kernels for 0% -> 0%
where the time goes in v1:
time: 94.6 us; the launch traced here: 94.3 us
  Pallas kernels  91 us (96%)
  local copies, waits for them, and re-layouts  2.64 us (3%)
    pallas_call x1, Pallas kernels, body(): pl.pallas_call(functools.partial(kernel, (groups, devs, rounds, seeds, ro...  91 us
    unnamed x2, local copies, waits for them, and re-layouts  2.64 us

profile of v1, /device:TPU:0, one launch (start us, length us, event | category | flops | bytes accessed | tf_op | source)
XLA Modules:
  0.0 94.3 jit_solution(320288109040121135)
XLA Ops:
  0.6 91.0 %seed_rounds.1 = (f32[64,128]{1,0:T(8,128)}, f32[8,128]{1,0:T(8,128)}) custom-call(s32[6,512]{1,0:T(8,128)} %ids.1, f32[64,128]{1,0:T(8,128)} %bitcast.3, bf16[8192,256]{1,0:T(8,128)(2,1)} %e_hbm.1), custom_call_target="tpu_custom_call" | custom-call | tf_op jit(solution)/shard_map/seed_rounds/pallas_call | solution.py:261
  91.7 1.3 %copy.5 = f32[6,1]{0,1:T(1,128)} copy(f32[6,1]{1,0:T(8,128)} %bitcast.5) | data formatting | bytes 48
  92.9 1.4 %copy.7 = f32[8192]{0:T(1024)} copy(f32[8192]{0:T(1024)} %bitcast.4) | data formatting | bytes 65536

commit v2 on v1

--- a/solution.py
+++ b/solution.py
@@ -10,6 +10,7 @@
 MESH = pl.DeviceIdType.MESH
 LOAD_CHUNKS = 8
 TILE = 256
+WIDE = 2048
 NT = (((1,), (1,)), ((), ()))
 
 
@@ -133,14 +134,15 @@
 
     ones_row = jnp.ones((8, width), jnp.bfloat16)
 
-    @pl.loop(0, rows // TILE)
+    @pl.loop(0, rows // WIDE)
     def _(t):
-        at = pl.ds(pl.multiple_of(t * TILE, TILE), TILE)
-        high, low = split_square(ef[at, :])
-        total = lax.dot_general(ones_row, high, NT, preferred_element_type=jnp.float32)
-        total += lax.dot_general(ones_row, low, NT, preferred_element_type=jnp.float32)
-        for q in range(TILE // 128):
-            rn[t * (TILE // 128) + q] = total[:, q * 128 : (q + 1) * 128]
+        for j in range(WIDE // TILE):
+            high, low = split_square(ef[pl.ds(pl.multiple_of(t * WIDE + j * TILE, TILE), TILE), :])
+            total = lax.dot_general(ones_row, high, NT, preferred_element_type=jnp.float32)
+            total += lax.dot_general(ones_row, low, NT, preferred_element_type=jnp.float32)
+            for q in range(TILE // 128):
+                at = t * (WIDE // 128) + j * (TILE // 128) + q
+                rn[at] = total[:, q * 128 : (q + 1) * 128]
 
     for k in range(slots):
         def reduce_chips(k=k):
@@ -173,16 +175,19 @@
         norms += jnp.dot(low, ones_col, preferred_element_type=jnp.float32)
         snb[...] = 0.5 * norms
 
-        @pl.loop(0, rows // TILE)
+        @pl.loop(0, rows // WIDE)
         def _(t):
-            at = pl.multiple_of(t * TILE, TILE)
-            block = e[pl.ds(at, TILE), :]
-            products = lax.dot_general(
-                cent[r].reshape(seeds, width), block, NT, preferred_element_type=jnp.float32
-            )
-            for q in range(TILE // 128):
-                score = products[:, q * 128 : (q + 1) * 128] - snb[...]
-                hm[r, t * (TILE // 128) + q] = jnp.max(score.reshape(seeds // 8, 8, 128), axis=0)
+            for j in range(WIDE // TILE):
+                at = pl.multiple_of(t * WIDE + j * TILE, TILE)
+                products = lax.dot_general(
+                    cent[r].reshape(seeds, width), e[pl.ds(at, TILE), :], NT,
+                    preferred_element_type=jnp.float32,
+                )
+                for q in range(TILE // 128):
+                    score = products[:, q * 128 : (q + 1) * 128] - snb[...]
+                    hm[r, t * (WIDE // 128) + j * (TILE // 128) + q] = jnp.max(
+                        score.reshape(seeds // 8, 8, 128), axis=0
+                    )
 
     items = [(k, o) for k in range(slots) for o in range(groups)]
 

time: 94.6 us -> 59.8 us (0.63)
  Pallas kernels: 91 us -> 56.2 us
    pallas_call x1, Pallas kernels: 91 us -> 56.2 us  [body(): pl.pallas_call(functools.partial(kernel, (groups, devs, rounds, seeds, ro...]
where the time goes in v2:
time: 59.8 us; the launch traced here: 59.4 us
  Pallas kernels  56.2 us (94%)
  local copies, waits for them, and re-layouts  2.64 us (4%)
  between operations  0.64 us (1%)
    pallas_call x1, Pallas kernels, body(): pl.pallas_call(functools.partial(kernel, (groups, devs, rounds, seeds, ro...  56.2 us
    unnamed x2, local copies, waits for them, and re-layouts  2.64 us

profile of v2, /device:TPU:0, one launch (start us, length us, event | category | flops | bytes accessed | tf_op | source)
XLA Modules:
  0.0 59.4 jit_solution(16082381366649257104)
XLA Ops:
  0.6 56.2 %seed_rounds.1 = (f32[64,128]{1,0:T(8,128)}, f32[8,128]{1,0:T(8,128)}) custom-call(s32[6,512]{1,0:T(8,128)} %ids.1, f32[64,128]{1,0:T(8,128)} %bitcast.3, bf16[8192,256]{1,0:T(8,128)(2,1)} %e_hbm.1), custom_call_target="tpu_custom_call" | custom-call | tf_op jit(solution)/shard_map/seed_rounds/pallas_call | solution.py:266
  56.8 1.3 %copy.5 = f32[6,1]{0,1:T(1,128)} copy(f32[6,1]{1,0:T(8,128)} %bitcast.5) | data formatting | bytes 48
  58.1 1.4 %copy.7 = f32[8192]{0:T(1024)} copy(f32[8192]{0:T(1024)} %bitcast.4) | data formatting | bytes 65536

commit v3 on v2

--- a/solution.py
+++ b/solution.py
@@ -60,9 +60,9 @@
     for i in range(LOAD_CHUNKS):
         load(i).wait()
 
-        @pl.loop(0, chunk // 64)
+        @pl.loop(0, chunk // 256)
         def _(t):
-            at = pl.ds(pl.multiple_of(i * chunk + t * 64, 64), 64)
+            at = pl.ds(pl.multiple_of(i * chunk + t * 256, 256), 256)
             ef[at, :] = e[at, :].astype(jnp.float32)
 
     def gather(slot, which, dst):
@@ -110,42 +110,39 @@
         else:
             pl.when(peer(o) + groups * k < rounds)(f)
 
-    first = True
-    for k in range(slots):
-        def start_slot(k=k, first=first):
+    def start_slot(k):
+        def f():
             gather(k, 1 - h, out_half)
-            if first:
+            if k == 0:
                 pl.semaphore_wait(barrier, devs - 1 + groups - 1)
             to_partner(k).start()
             gather(k, h, own_half)
-
-        if_held(k, 0, start_slot)
-        first = False
-
-    for k in range(slots):
-        def reduce_pair(k=k):
             to_partner(k).wait_recv()
             both = own_half[k] + pin[k]
             half[k] = both.reshape(chips, piece, width)
             for o in range(1, chips):
                 scatter(k, o).start()
 
-        if_held(k, 0, reduce_pair)
+        if_held(k, 0, f)
+
+    for k in range(slots):
+        start_slot(k)
 
     ones_row = jnp.ones((8, width), jnp.bfloat16)
 
-    @pl.loop(0, rows // WIDE)
-    def _(t):
-        for j in range(WIDE // TILE):
-            high, low = split_square(ef[pl.ds(pl.multiple_of(t * WIDE + j * TILE, TILE), TILE), :])
-            total = lax.dot_general(ones_row, high, NT, preferred_element_type=jnp.float32)
-            total += lax.dot_general(ones_row, low, NT, preferred_element_type=jnp.float32)
-            for q in range(TILE // 128):
-                at = t * (WIDE // 128) + j * (TILE // 128) + q
-                rn[at] = total[:, q * 128 : (q + 1) * 128]
-
-    for k in range(slots):
-        def reduce_chips(k=k):
+    def row_norms(first, last):
+        @pl.loop(first, last)
+        def _(t):
+            for j in range(WIDE // TILE):
+                high, low = split_square(ef[pl.ds(pl.multiple_of(t * WIDE + j * TILE, TILE), TILE), :])
+                total = lax.dot_general(ones_row, high, NT, preferred_element_type=jnp.float32)
+                total += lax.dot_general(ones_row, low, NT, preferred_element_type=jnp.float32)
+                for q in range(TILE // 128):
+                    at = t * (WIDE // 128) + j * (TILE // 128) + q
+                    rn[at] = total[:, q * 128 : (q + 1) * 128]
+
+    def reduce_chips(k):
+        def f():
             total = half[k, c]
             for o in range(1, chips):
                 scatter(k, o).wait_recv()
@@ -154,17 +151,26 @@
             for o in range(1, chips):
                 spread(k, o).start()
 
-        if_held(k, 0, reduce_chips)
-
-    for k in range(slots):
-        def share(k=k):
+        if_held(k, 0, f)
+
+    def share(k):
+        def f():
             for o in range(1, chips):
                 spread(k, o).wait_recv()
             for o in range(1, groups):
                 across(k, o).start()
             forward(k, 0).start()
 
-        if_held(k, 0, share)
+        if_held(k, 0, f)
+
+    steps = rows // WIDE
+    parts_of = [steps * i // (slots + 1) for i in range(slots + 2)]
+    for k in range(slots):
+        row_norms(parts_of[k], parts_of[k + 1])
+        reduce_chips(k)
+    row_norms(parts_of[slots], steps)
+    for k in range(slots):
+        share(k)
 
     ones_col = jnp.ones((width, 128), jnp.bfloat16)
 
@@ -189,7 +195,8 @@
                         score.reshape(seeds // 8, 8, 128), axis=0
                     )
 
-    items = [(k, o) for k in range(slots) for o in range(groups)]
+    items = [(k, 0) for k in range(slots)]
+    items += [(k, o) for k in range(slots) for o in range(1, groups)]
 
     def relay(k, o):
         def f():
@@ -207,7 +214,9 @@
         if_held(k, o, f)
 
     for n, (k, o) in enumerate(items):
-        if n + 1 < len(items):
+        if n == slots:
+            relay(k, o)
+        if n >= slots and n + 1 < len(items):
             relay(*items[n + 1])
         finish(k, o)
 

time: 59.8 us -> 54.7 us (0.915)
  Pallas kernels: 56.2 us -> 50.6 us
    pallas_call x1, Pallas kernels: 56.2 us -> 50.6 us  [body(): pl.pallas_call(functools.partial(kernel, (groups, devs, rounds, seeds, ro...]
where the time goes in v3:
time: 54.7 us; the launch traced here: 53.9 us
  Pallas kernels  50.6 us (93%)
  local copies, waits for them, and re-layouts  2.64 us (5%)
  between operations  0.64 us (1%)
    pallas_call x1, Pallas kernels, body(): pl.pallas_call(functools.partial(kernel, (groups, devs, rounds, seeds, ro...  50.6 us
    unnamed x2, local copies, waits for them, and re-layouts  2.64 us

profile of v3, /device:TPU:0, one launch (start us, length us, event | category | flops | bytes accessed | tf_op | source)
XLA Modules:
  0.0 53.9 jit_solution(15776688996037846271)
XLA Ops:
  0.6 50.6 %seed_rounds.1 = (f32[64,128]{1,0:T(8,128)}, f32[8,128]{1,0:T(8,128)}) custom-call(s32[6,512]{1,0:T(8,128)} %ids.1, f32[64,128]{1,0:T(8,128)} %bitcast.3, bf16[8192,256]{1,0:T(8,128)(2,1)} %e_hbm.1), custom_call_target="tpu_custom_call" | custom-call | tf_op jit(solution)/shard_map/seed_rounds/pallas_call | solution.py:275
  51.2 1.3 %copy.5 = f32[6,1]{0,1:T(1,128)} copy(f32[6,1]{1,0:T(8,128)} %bitcast.5) | data formatting | bytes 48
  52.5 1.4 %copy.7 = f32[8192]{0:T(1024)} copy(f32[8192]{0:T(1024)} %bitcast.4) | data formatting | bytes 65536
